TPU v7x, 32 devices: a 4x4x1 block of a 4x4x8 slice. The times are simulated.
32 devices in a mesh: data: 1 (over z), cp: 4 (over y), tp: 8 (over x, core).
Axes of the slice: x: 4, y: 4, z: 1, core: 2. Of those that a mesh axis runs over, the one named last changes fastest.
The devices are a block of a 4x4x8 slice.
Arguments:
- act_in: bfloat16 [2, 2048, 1536], P(None, ('data', 'cp', 'tp'))
- route_ids: int32 [2, 2048, 2], P(None, ('data', 'cp', 'tp'))
- route_gates: float32 [2, 2048, 2], P(None, ('data', 'cp', 'tp'))
- w_query: bfloat16 [1536, 24, 64], P(None, 'tp')
- w_key: bfloat16 [1536, 8, 64], P(None, 'tp')
- w_value: bfloat16 [1536, 8, 64], P(None, 'tp')
- w_out: bfloat16 [24, 64, 1536], P('tp')
- w_gate: bfloat16 [32, 1536, 512], P(('cp', 'tp'))
- w_up: bfloat16 [32, 1536, 512], P(('cp', 'tp'))
- w_down: bfloat16 [32, 512, 1536], P(('cp', 'tp'))
Outputs:
- output: bfloat16 [2, 2048, 1536], P(None, ('data', 'cp', 'tp'))
All inputs are finite; a program needn't handle non-finite values.
Results may differ from a plain program's by a relative error of at most 0.00477921.
Values are sent between devices in bfloat16 or wider.
A program may use at most 768 MiB of HBM per device.

v0:
```python
import jax
import jax.numpy as jnp
from jax import lax
from jax.sharding import PartitionSpec as P


def pick_rows(row_table, row_ids):
    return jnp.take(row_table, row_ids, axis=0, mode='fill', fill_value=0)


def attend_local(act_in, w_query, w_key, w_value, w_out, cp_size, tp_size):
    n_micro, tokens, hidden = act_in.shape
    q_local, head_dim = w_query.shape[1], w_query.shape[2]
    kv_local = w_key.shape[1]
    group_size = q_local // kv_local
    half_rows = tokens * tp_size
    piece_len = half_rows // 2
    seq_len = half_rows * cp_size
    cp_rank = lax.axis_index('cp')
    x_half = lax.all_gather(act_in, 'tp', axis=1, tiled=True)
    query_rows = jnp.einsum('bsh,hnd->bsnd', x_half, w_query, preferred_element_type=jnp.float32).astype(jnp.bfloat16)
    query_rows = query_rows.reshape(n_micro, half_rows, kv_local, group_size, head_dim)
    key_half = jnp.einsum('bsh,hnd->bsnd', x_half, w_key, preferred_element_type=jnp.float32).astype(jnp.bfloat16)
    value_half = jnp.einsum('bsh,hnd->bsnd', x_half, w_value, preferred_element_type=jnp.float32).astype(jnp.bfloat16)
    key_all = lax.all_gather(key_half, 'cp', axis=1, tiled=True)
    value_all = lax.all_gather(value_half, 'cp', axis=1, tiled=True)
    local_ix = jnp.arange(half_rows)
    owner_ix = jnp.arange(cp_size)[:, None]
    key_pos = jnp.where(local_ix < piece_len, owner_ix * piece_len + local_ix, (2 * cp_size - 1 - owner_ix) * piece_len + local_ix - piece_len).reshape(seq_len)
    score_scale = head_dim ** -0.5
    halves = []
    for half_id in range(2):
        piece_id = cp_rank if half_id == 0 else 2 * cp_size - 1 - cp_rank
        query_pos = piece_id * piece_len + jnp.arange(piece_len)
        q_part = query_rows[:, half_id * piece_len:(half_id + 1) * piece_len]
        scores = jnp.einsum('bqhgd,bkhd->bhgqk', q_part, key_all, preferred_element_type=jnp.float32) * score_scale
        scores = jnp.where(key_pos[None, :] <= query_pos[:, None], scores, -jnp.inf)
        row_peak = jnp.max(scores, axis=-1, keepdims=True)
        exp_scores = jnp.exp(scores - row_peak)
        row_sum = jnp.sum(exp_scores, axis=-1)
        weighted = jnp.einsum('bhgqk,bkhd->bqhgd', exp_scores.astype(jnp.bfloat16), value_all, preferred_element_type=jnp.float32)
        weighted = weighted / jnp.transpose(row_sum, (0, 3, 1, 2))[..., None]
        halves.append(weighted.astype(jnp.bfloat16))
    attn_rows = jnp.concatenate(halves, axis=1).reshape(n_micro, half_rows, q_local, head_dim)
    partial = jnp.einsum('bsnd,ndh->bsh', attn_rows, w_out, preferred_element_type=jnp.float32)
    attn_sum = lax.psum_scatter(partial, 'tp', scatter_dimension=1, tiled=True)
    return (act_in.astype(jnp.float32) + attn_sum).astype(jnp.bfloat16)


def dispatch_experts(mid_rows, route_ids, route_gates, w_gate, w_up, w_down, experts):
    n_micro, tokens, hidden = mid_rows.shape
    capacity = (4 * tokens) // experts
    flat_ids = route_ids.reshape(n_micro, 2 * tokens)
    expert_hits = (flat_ids[..., None] == jnp.arange(experts)).astype(jnp.int32)
    slot_rank = jnp.sum((jnp.cumsum(expert_hits, axis=1) - 1) * expert_hits, axis=-1)
    dest_slot = flat_ids * capacity + slot_rank
    micro_ix = jnp.arange(n_micro)[:, None]
    token_of = jnp.broadcast_to((jnp.arange(2 * tokens, dtype=jnp.int32) // 2)[None, :], dest_slot.shape)
    source_row = jnp.full((n_micro, experts * capacity), tokens, jnp.int32).at[micro_ix, dest_slot].set(token_of)
    send_buf = jax.vmap(pick_rows)(mid_rows, source_row).reshape(n_micro, experts, capacity, hidden)
    recv_buf = lax.all_to_all(send_buf, ('cp', 'tp'), 1, 1, tiled=True)
    expert_in = recv_buf.reshape(n_micro, experts * capacity, hidden)
    gate_act = jnp.einsum('bth,hf->btf', expert_in, w_gate[0], preferred_element_type=jnp.float32)
    up_act = jnp.einsum('bth,hf->btf', expert_in, w_up[0], preferred_element_type=jnp.float32)
    mixed_act = (jax.nn.silu(gate_act) * up_act).astype(jnp.bfloat16)
    expert_out = jnp.einsum('btf,fh->bth', mixed_act, w_down[0], preferred_element_type=jnp.float32).astype(jnp.bfloat16)
    back_buf = lax.all_to_all(expert_out.reshape(n_micro, experts, capacity, hidden), ('cp', 'tp'), 1, 1, tiled=True)
    picked = jax.vmap(pick_rows)(back_buf.reshape(n_micro, experts * capacity, hidden), dest_slot).reshape(n_micro, tokens, 2, hidden)
    combined = route_gates[:, :, 0:1] * picked[:, :, 0].astype(jnp.float32) + route_gates[:, :, 1:2] * picked[:, :, 1].astype(jnp.float32)
    return (mid_rows.astype(jnp.float32) + combined).astype(jnp.bfloat16)


def solution(mesh):
    cp_size = mesh.shape['cp']
    tp_size = mesh.shape['tp']
    experts = cp_size * tp_size
    row_spec = P(None, ('data', 'cp', 'tp'), None)
    head_spec = P(None, 'tp', None)
    out_spec = P('tp', None, None)
    expert_spec = P(('cp', 'tp'), None, None)

    def device_step(act_in, route_ids, route_gates, w_query, w_key, w_value, w_out, w_gate, w_up, w_down):
        mid_rows = attend_local(act_in, w_query, w_key, w_value, w_out, cp_size, tp_size)
        return dispatch_experts(mid_rows, route_ids, route_gates, w_gate, w_up, w_down, experts)

    return jax.shard_map(device_step, mesh=mesh, in_specs=(row_spec, row_spec, row_spec, head_spec, head_spec, head_spec, out_spec, expert_spec, expert_spec, expert_spec), out_specs=row_spec, check_vma=False)
```

profile of v0, /device:TPU:97, one launch (start us, length us, event | category | flops | bytes accessed | tf_op | source)
XLA Modules:
  0.0 232.4 jit_solution(1646899270769205646)
XLA Ops:
  8.3 30.0 %all-gather.4.cloned.1.call-done = bf16[2,512,1536]{2,1,0:T(8,128)(2,1)} async-done(((bf16[2,64,1536]{2,1,0:T(8,128)(2,1)}), bf16[2,512,1536]{2,1,0:T(8,128)(2,1)}) %all-gather.4.cloned.1.call-update) | async-done | bytes 3145744 | tf_op jit(solution)/shard_map/all_gather | solution.py:20
  38.2 3.1 %convolution_convert_fusion.2 = bf16[2,512,64]{1,2,0:T(8,128)(2,1)S(1)} fusion(bf16[2,512,1536]{2,1,0:T(8,128)(2,1)} %all-gather.4.cloned.1.call-done, bf16[1536,1,64]{0,2,1:T(8,128)(2,1)} %param.15), kind=kOutput, calls=%fused_computation.42 | convolution fusion | flops 201392128 | bytes 3473408 | tf_op jit(solution)/shard_map/bsh,hnd->bsnd/dot_general | solution.py:24
  41.3 11.3 %all-gather = bf16[2,2048,64]{1,2,0:T(8,128)(2,1)S(1)} all-gather(bf16[2,512,64]{1,2,0:T(8,128)(2,1)S(1)} %convolution_convert_fusion.2), channel_id=2, replica_groups=mesh['data'=1,'cp'=4,'tp'=8] {'cp'}, dimensions={1}, use_global_device_ids=true | all-gather | bytes 655360 | tf_op jit(solution)/shard_map/all_gather | solution.py:26
  53.7 9.9 %all-gather.1 = bf16[2,2048,64]{1,2,0:T(8,128)(2,1)S(1)} all-gather(bf16[2,512,64]{1,2,0:T(8,128)(2,1)S(1)} %convolution_convert_fusion.1), channel_id=3, replica_groups=mesh['data'=1,'cp'=4,'tp'=8] {'cp'}, dimensions={1}, use_global_device_ids=true | all-gather | bytes 655360 | tf_op jit(solution)/shard_map/all_gather | solution.py:25
  64.8 6.6 %fusion.4 = (f32[2,3,256]{2,1,0:T(4,128)S(1)}, f32[2,2048,256,3]{2,1,3,0:T(8,128)}) fusion(pred[256,2048]{0,1:T(8,128)(4,1)S(1)} %get-tuple-element.5, bf16[2,512,1,3,64]{1,4,3,0,2:T(8,128)(2,1)S(1)} %fusion.45, bf16[2,2048,64]{1,2,0:T(8,128)(2,1)S(1)} %all-gather.1), kind=kOutput, calls=%fused_computation.11 | convolution fusion | flops 412088832 | bytes 13834240 | tf_op jit(solution)/shard_map/bqhgd,bkhd->bhgqk/dot_general | solution.py:36
  71.4 2.1 fusion.5
  73.5 7.2 %fusion = f32[2,3,256]{2,1,0:T(4,128)S(1)} fusion(f32[2,2048,256,3]{2,1,3,0:T(8,128)} %get-tuple-element.14, f32[2,3,256]{2,1,0:T(4,128)S(1)} %get-tuple-element.13, pred[256,2048]{0,1:T(8,128)(4,1)S(1)} %get-tuple-element.5), kind=kLoop, calls=%fused_computation.7 | loop fusion | flops 12581376 | bytes 13119488 | tf_op jit(solution)/shard_map/reduce_sum | solution.py:40
  80.7 6.4 %fusion.51 = bf16[2,256,1,3,64]{1,4,3,0,2:T(8,128)(2,1)S(1)} fusion(f32[2,2048,256,3]{2,1,3,0:T(8,128)} %get-tuple-element.14, f32[2,3,256]{2,1,0:T(4,128)S(1)} %get-tuple-element.13, pred[256,2048]{0,1:T(8,128)(4,1)S(1)} %get-tuple-element.5, bf16[2,2048,64]{1,2,0:T(8,128)(2,1)S(1)} %all-gather, f32[2,256,3]{1,2,0:T(4,128)S(1)} %bitcast.221), kind=kOutput, calls=%fused_computation.46 | convolution fusion | flops 415432704 | bytes 13840384 | tf_op jit(solution)/shard_map/bhgqk,bkhd->bqhgd/dot_general | solution.py:41
  87.1 2.6 %fusion.2 = f32[2,3,256]{2,1,0:T(4,128)S(1)} fusion(f32[2,2048,256,3]{2,1,3,0:T(8,128)S(1)} %get-tuple-element.12, f32[2,3,256]{2,1,0:T(4,128)S(1)} %get-tuple-element.11, pred[256,2048]{0,1:T(8,128)(4,1)S(1)} %get-tuple-element.6), kind=kLoop, calls=%fused_computation.9 | loop fusion | flops 12581376 | bytes 13119488 | tf_op jit(solution)/shard_map/reduce_sum | solution.py:40
  89.7 3.4 %fusion.57 = bf16[2,256,1,3,64]{1,4,3,0,2:T(8,128)(2,1)S(1)} fusion(f32[2,2048,256,3]{2,1,3,0:T(8,128)S(1)} %get-tuple-element.12, f32[2,3,256]{2,1,0:T(4,128)S(1)} %get-tuple-element.11, pred[256,2048]{0,1:T(8,128)(4,1)S(1)} %get-tuple-element.6, bf16[2,2048,64]{1,2,0:T(8,128)(2,1)S(1)} %all-gather, f32[2,256,3]{1,2,0:T(4,128)S(1)} %bitcast.220), kind=kOutput, calls=%fused_computation.48 | convolution fusion | flops 415432704 | bytes 13840384 | tf_op jit(solution)/shard_map/bhgqk,bkhd->bqhgd/dot_general | solution.py:41
  93.1 3.7 %convolution_bitcast_fusion = f32[2,512,1536]{2,1,0:T(8,128)} fusion(bf16[3,64,1536]{2,1,0:T(8,128)(2,1)S(1)} %copy-done.3, bf16[2,256,1,3,64]{1,4,3,0,2:T(8,128)(2,1)S(1)} %fusion.57, bf16[2,256,1,3,64]{1,4,3,0,2:T(8,128)(2,1)S(1)} %fusion.51), kind=kOutput, calls=%fused_computation.19 | convolution fusion | flops 604766208 | bytes 7274496 | tf_op jit(solution)/shard_map/bsnd,ndh->bsh/dot_general | solution.py:45
  98.5 12.5 %scatter_fusion = s32[2,256]{1,0:T(2,128)S(1)} fusion(s32[2,256]{1,0:T(2,128)S(1)} %broadcast_in_dim.73, s32[256]{0:T(256)S(1)} %get-tuple-element.10, s32[256]{0:T(256)S(1)} %broadcast_bitcast_fusion), kind=kCustom, calls=%fused_computation.2 | custom fusion | bytes 5120 | tf_op jit(solution)/shard_map/scatter | solution.py:59
  111.7 29.5 %reduce-scatter.2.cloned.1.call-done = f32[2,64,1536]{2,1,0:T(8,128)} async-done(((f32[2,512,1536]{2,1,0:T(8,128)}), f32[2,64,1536]{2,1,0:T(8,128)}) %reduce-scatter.2.cloned.1.call-update) | async-done | bytes 786448 | tf_op jit(solution)/shard_map/reduce_scatter | solution.py:46
  141.2 1.2 add_convert_fusion
  142.4 6.9 %gather_fusion = bf16[512,1536]{1,0:T(8,128)(2,1)S(1)} fusion(bf16[2,64,1536]{2,1,0:T(8,128)(2,1)S(1)} %add_convert_fusion, s32[512]{0:T(512)S(1)} %bitcast.217), kind=kCustom, calls=%fused_computation | custom fusion | bytes 3149824 | tf_op jit(solution)/shard_map/vmap(jit(_take))/gather | solution.py:8
  150.4 28.2 %all_to_all.10 = bf16[2,32,8,1536]{3,2,0,1:T(8,128)(2,1)S(1)} all-to-all(bf16[2,32,8,1536]{3,2,0,1:T(8,128)(2,1)S(1)} %copy_select_fusion), channel_id=1, replica_groups=mesh['data'=1,'cp'=4,'tp'=8] {'cp','tp'}, dimensions={1} | all-to-all | bytes 3145728 | tf_op jit(solution)/shard_map/all_to_all | solution.py:61
  178.6 2.0 fusion.20
  180.6 4.7 %fusion.16 = bf16[2,32,8,1536]{3,2,1,0:T(8,128)(2,1)} fusion(bf16[1,512,1536]{2,1,0:T(8,128)(2,1)S(1)} %copy-done, bf16[1,1536,512]{2,1,0:T(8,128)(2,1)} %param.18, bf16[2,32,8,1536]{3,2,0,1:T(8,128)(2,1)S(1)} %all_to_all.10, f32[2,256,512]{2,1,0:T(8,128)} %fusion.20), kind=kOutput, calls=%fused_computation.23 | convolution fusion | flops 1612972032 | bytes 7340032 | tf_op jit(solution)/shard_map/btf,fh->bth/dot_general | solution.py:66
  185.3 2.8 %copy.40 = bf16[2,32,8,1536]{3,2,0,1:T(8,128)(2,1)} copy(bf16[2,32,8,1536]{3,2,1,0:T(8,128)(2,1)} %fusion.16) | data formatting | bytes 3145728 | tf_op jit(solution)/shard_map/reshape | solution.py:67
  188.1 4.0 %all-to-all-start.1 = ((bf16[2,32,8,1536]{3,2,0,1:T(8,128)(2,1)}), bf16[2,32,8,1536]{3,2,0,1:T(8,128)(2,1)}, u32[]{:S(2)}, u32[]{:S(2)}) async-start(bf16[2,32,8,1536]{3,2,0,1:T(8,128)(2,1)} %copy.40), calls=%async_computation.2 | async-start | bytes 3145728 | tf_op jit(solution)/shard_map/all_to_all | solution.py:67
  192.3 24.0 %all-to-all-done.1 = bf16[2,32,8,1536]{3,2,0,1:T(8,128)(2,1)} async-done(((bf16[2,32,8,1536]{3,2,0,1:T(8,128)(2,1)}), bf16[2,32,8,1536]{3,2,0,1:T(8,128)(2,1)}, u32[]{:S(2)}, u32[]{:S(2)}) %all-to-all-start.1) | async-done | bytes 1572896 | tf_op jit(solution)/shard_map/all_to_all | solution.py:67
  216.4 1.5 copy.68
  217.9 4.4 %gather_fusion.1 = bf16[256,1536]{1,0:T(8,128)(2,1)} fusion(bf16[2,256,1536]{2,1,0:T(8,128)(2,1)S(1)} %bitcast.216, s32[256]{0:T(256)S(1)} %get-tuple-element.9), kind=kCustom, calls=%fused_computation.1 | custom fusion | bytes 1574912 | tf_op jit(solution)/shard_map/vmap(jit(_take))/gather | solution.py:8
  222.3 2.2 gather.15
  (55 shorter events, 8.7 us)
Async XLA Ops:
  6.5 174.0 %copy-start = (bf16[1,512,1536]{2,1,0:T(8,128)(2,1)S(1)}, bf16[1,512,1536]{2,1,0:T(8,128)(2,1)}, u32[]{:S(2)}) copy-start(bf16[1,512,1536]{2,1,0:T(8,128)(2,1)} %param.19) | copy-start | bytes 4718596
  6.6 46.1 %copy-start.4 = (bf16[1536,1,64]{0,2,1:T(8,128)(2,1)S(1)}, bf16[1536,1,64]{0,2,1:T(8,128)(2,1)}, u32[]{:S(2)}) copy-start(bf16[1536,1,64]{0,2,1:T(8,128)(2,1)} %param.14) | copy-start | bytes 589828
  6.6 31.7 %all-gather.4.cloned.1.call-start = ((), (), s32[]{:S(2)}) async-start(), calls=%async_computation.3 | async-start | bytes 3538944 | tf_op jit(solution)/shard_map/all_gather | solution.py:20
  7.3 133.9 %reduce-scatter.2.cloned.1.call-start = ((), (), s32[]{:S(2)}) async-start(), calls=%async_computation.4 | async-start | bytes 7077888 | tf_op jit(solution)/shard_map/reduce_scatter | solution.py:46
  38.2 14.4 %copy-start.1 = (bf16[2,512,1536]{2,1,0:T(8,128)(2,1)S(1)}, bf16[2,512,1536]{2,1,0:T(8,128)(2,1)}, u32[]{:S(2)}) copy-start(bf16[2,512,1536]{2,1,0:T(8,128)(2,1)} %all-gather.4.cloned.1.call-done) | copy-start | bytes 9437188
  41.3 22.3 %copy-start.8 = (bf16[1536,3,64]{0,2,1:T(8,128)(2,1)S(1)}, bf16[1536,3,64]{0,2,1:T(8,128)(2,1)}, u32[]{:S(2)}) copy-start(bf16[1536,3,64]{0,2,1:T(8,128)(2,1)} %param.13) | copy-start | bytes 1769476
  89.7 3.4 %copy-start.3 = (bf16[3,64,1536]{2,1,0:T(8,128)(2,1)S(1)}, bf16[3,64,1536]{2,1,0:T(8,128)(2,1)}, u32[]{:S(2)}) copy-start(bf16[3,64,1536]{2,1,0:T(8,128)(2,1)} %param.16) | copy-start | bytes 1769476
  96.7 0.7 copy-start.5
  96.7 44.4 %copy-start.2 = (bf16[2,64,1536]{2,1,0:T(8,128)(2,1)S(1)}, bf16[2,64,1536]{2,1,0:T(8,128)(2,1)}, u32[]{:S(2)}) copy-start(bf16[2,64,1536]{2,1,0:T(8,128)(2,1)} %param.10) | copy-start | bytes 1179652
  149.3 29.2 %copy-start.7 = (bf16[1,1536,512]{2,1,0:T(8,128)(2,1)S(1)}, bf16[1,1536,512]{2,1,0:T(8,128)(2,1)}, u32[]{:S(2)}) copy-start(bf16[1,1536,512]{2,1,0:T(8,128)(2,1)} %param.17) | copy-start | bytes 4718596
  185.3 7.0 %copy-start.6 = (f32[2,64,2]{1,2,0:T(2,128)S(1)}, f32[2,64,2]{1,2,0:T(2,128)}, u32[]{:S(2)}) copy-start(f32[2,64,2]{1,2,0:T(2,128)} %param.12) | copy-start | bytes 3076
  188.1 28.3 %all-to-all-start.1 = ((bf16[2,32,8,1536]{3,2,0,1:T(8,128)(2,1)}), bf16[2,32,8,1536]{3,2,0,1:T(8,128)(2,1)}, u32[]{:S(2)}, u32[]{:S(2)}) async-start(bf16[2,32,8,1536]{3,2,0,1:T(8,128)(2,1)} %copy.40), calls=%async_computation.2 | async-start | bytes 3145728 | tf_op jit(solution)/shard_map/all_to_all | solution.py:67
Sparse Core Ops, SparseCore 0:
  8.9 29.2 all-gather.3
  96.9 44.1 reduce-scatter.1
where the time goes:
time: 233 us; the launch traced here: 232 us
  waiting for transfers between devices  84.2 us (36%)
  blocking collectives  49.5 us (21%)
  matrix products  34.1 us (15%)
  local copies, waits for them, and re-layouts  32.4 us (14%)
  other arithmetic  14.5 us (6%)
  between operations  13.7 us (6%)
  starting transfers between devices  4.06 us (2%)
    all_gather x1, waiting for transfers between devices, attend_local(): x_half = lax.all_gather(act_in, 'tp', axis=1, tiled=True)  30 us
    reduce_scatter x1, waiting for transfers between devices, attend_local(): attn_sum = lax.psum_scatter(partial, 'tp', scatter_dimension=1, tiled=True)  29.5 us
    all_to_all x1, blocking collectives, dispatch_experts(): recv_buf = lax.all_to_all(send_buf, ('cp', 'tp'), 1, 1, tiled=True)  28.2 us
    all_to_all x1, waiting for transfers between devices, dispatch_experts(): lax.all_to_all(expert_out.reshape(n_micro, experts, capacity, hidden), ('...  24 us
    gather x3, local copies, waits for them, and re-layouts, pick_rows(): return jnp.take(row_table, row_ids, axis=0, mode='fill', fill_value=0)  13.5 us
    scatter x1, local copies, waits for them, and re-layouts, dispatch_experts(): jnp.full((n_micro, experts * capacity), tokens, jnp.int32)  12.5 us
    all_gather x1, blocking collectives, attend_local(): value_all = lax.all_gather(value_half, 'cp', axis=1, tiled=True)  11.3 us
    all_gather x1, blocking collectives, attend_local(): key_all = lax.all_gather(key_half, 'cp', axis=1, tiled=True)  9.95 us
  transfers between devices with their start and end apart: 3, of which 3 were waited for; matrix products, arithmetic and copies ran while one was open for 7% of the time, Pallas kernels for 0%

commit v1 on v0

v1 whole, which is shorter than its diff:
```python
import functools

import jax
import jax.numpy as jnp
from jax import lax
from jax.experimental import pallas as pl
from jax.experimental.pallas import tpu as pltpu
from jax.sharding import PartitionSpec as P

MESH = pl.DeviceIdType.MESH
F32 = jnp.float32
BF16 = jnp.bfloat16
NT = (((1,), (1,)), ((), ()))


def mm(a, b):
    return jnp.dot(a, b, preferred_element_type=F32)


def mm_nt(a, b):
    return lax.dot_general(a, b, NT, preferred_element_type=F32)


def layer_kernel(dims, x_hbm, ids_ref, gates_ref, wq_hbm, wk_hbm, wv_hbm, wo_hbm, wg_hbm, wu_hbm, wd_hbm, y_ref,
                 xf, wqkv, kv, qs, sbuf, mx, lsum, acc, osend, orecv, wof, onehot, onehot_t, gcol, hbuf,
                 dsend, drecv, rsend, rrecv, wg, wu, wd,
                 loc_sem, xs_sem, xr_sem, ws_sem, wr_sem, ks_sem, kr_sem, os_sem, or_sem,
                 ds_sem, dr_sem, rs_sem, rr_sem):
    cps, tps, seqs, n, hid, hd, qh, cap = dims
    experts = cps * tps
    group = experts
    chips = tps // 2
    hslots = tps // 2
    piece = n * hslots
    pieces = 2 * cps
    lanes = 2 * hd
    qrows = qh * piece
    kdim = qh * hd
    c = lax.axis_index('cp')
    t = lax.axis_index('tp')
    me = c * tps + t
    xc = t // 2
    core = t % 2

    def slot(dx, other):
        return ((xc + dx) % chips) * 2 + (core if not other else 1 - core)

    right, left, sib = slot(1, False), slot(chips - 1, False), slot(0, True)

    def rcopy(src, dst, ssem, rsem, cc, tt):
        return pltpu.make_async_remote_copy(src_ref=src, dst_ref=dst, send_sem=ssem, recv_sem=rsem,
                                            device_id={'cp': cc, 'tp': tt}, device_id_type=MESH)

    loads = []

    def load(src, dst, i):
        cp = pltpu.make_async_copy(src, dst, loc_sem.at[i])
        cp.start()
        loads.append(cp)
        return cp

    ld_x = [load(x_hbm.at[s], xf.at[s, t], s) for s in range(seqs)]
    ld_wo = load(wo_hbm, wof.at[t], 2)
    ld_qkv = [load(wv_hbm, wqkv.at[pl.ds(0, hd)], 3), load(wk_hbm, wqkv.at[pl.ds(hd, hd)], 4)]
    for i in range(qh):
        ld_qkv.append(load(wq_hbm.at[pl.ds(i * hd, hd)], wqkv.at[pl.ds(lanes * (i + 1) + hd, hd)], 5 + i))
    ld_exp = [load(wg_hbm, wg, 5 + qh), load(wu_hbm, wu, 6 + qh), load(wd_hbm, wd, 7 + qh)]

    barrier = pltpu.get_barrier_semaphore()

    def sig(i, _):
        g = (me + i) % group
        pl.semaphore_signal(barrier, inc=1, device_id={'cp': g // tps, 'tp': g % tps}, device_id_type=MESH)
        return 0

    lax.fori_loop(1, group, sig, 0)
    pl.semaphore_wait(barrier, group - 1)

    def gather_parts(buf, rows, ss, rs, chunked):
        half = rows // 2
        lo, hi = pl.ds(0, half), pl.ds(half, half)

        def ref(sl, part):
            return buf.at[sl] if part is None else buf.at[sl, part]

        def cp(src_slot, part, kind, dst):
            return rcopy(ref(src_slot, part), ref(src_slot, part), ss.at[kind], rs.at[kind], c, dst)

        nl, nr, op = slot(chips - 1, False), slot(1, False), slot(2, False)
        snl, snr, sop = slot(chips - 1, True), slot(1, True), slot(2, True)
        own = t
        sends = [
            (own, lo, right), (own, hi, right), (own, hi, left), (own, lo, left),
            (nl, lo, right), (nr, hi, left),
            (own, None, sib), (nl, None, sib), (nr, None, sib), (op, lo, sib), (op, hi, sib),
        ]
        gets = [
            (nl, lo), (nl, hi), (nr, hi), (nr, lo),
            (op, lo), (op, hi),
            (sib, None), (snl, None), (snr, None), (sop, lo), (sop, hi),
        ]

        def start(k):
            s_, p_, d_ = sends[k]
            cp(s_, p_, k, d_).start()

        def got(k):
            s_, p_ = gets[k]
            cp(s_, p_, k, sib).wait_recv()

        def sent(k):
            s_, p_, d_ = sends[k]
            cp(s_, p_, k, d_).wait_send()

        return start, got, sent

    xg = [gather_parts(xf.at[s], n, xs_sem.at[s], xr_sem.at[s], False) for s in range(seqs)]
    wg_parts = gather_parts(wof, kdim, ws_sem, wr_sem, True)

    for s in range(seqs):
        ld_x[s].wait()
        for k in (0, 2, 1, 3, 6):
            xg[s][0](k)

    ecol = lax.broadcasted_iota(jnp.int32, (experts, n), 0)
    later = (lax.broadcasted_iota(jnp.int32, (n, n), 0) < lax.broadcasted_iota(jnp.int32, (n, n), 1)).astype(F32).astype(BF16)
    srow = lax.broadcasted_iota(jnp.int32, (experts * cap, n), 0)
    eye = lax.broadcasted_iota(jnp.int32, (n, n), 0) == lax.broadcasted_iota(jnp.int32, (n, n), 1)
    for s in range(seqs):
        first = jnp.zeros((experts, 1), F32)
        both = None
        for k in range(2):
            idk = ids_ref[s, k:k + 1, :]
            hits = (ecol == idk).astype(F32)
            before = mm(hits.astype(BF16), later) + first
            rank = jnp.sum(hits * before, axis=0, keepdims=True).astype(jnp.int32)
            first = first + jnp.sum(hits, axis=1, keepdims=True)
            dest = idk * cap + rank
            pick = (srow == dest).astype(F32)
            both = pick if both is None else both + pick
            onehot_t[s, k * n:(k + 1) * n, :] = pick.T.astype(BF16)
            gcol[s, k] = jnp.broadcast_to(jnp.sum(jnp.where(eye, gates_ref[s, k:k + 1, :], 0.0), axis=1, keepdims=True), (n, 128))
        onehot[s] = both.astype(BF16)
    for i in range(qh):
        wqkv[lanes * (i + 1):lanes * (i + 1) + hd, :] = jnp.zeros((hd, hid), BF16)

    def relay(parts):
        start, got, sent = parts
        got(0)
        start(4)
        got(2)
        start(5)
        got(1)
        start(7)
        got(3)
        start(8)

    def finish(parts):
        start, got, sent = parts
        got(4)
        start(9)
        got(5)
        start(10)
        for k in (6, 7, 8, 9, 10):
            got(k)

    for s in range(seqs):
        relay(xg[s])
    ld_wo.wait()
    for k in (0, 2, 1, 3, 6):
        wg_parts[0](k)
    for cp in ld_qkv:
        cp.wait()

    def kv_piece(half):
        return c if half == 0 else pieces - 1 - c

    def kv_copy(s, half, r, src):
        ref = kv.at[s, src if half == 0 else pieces - 1 - src]
        return rcopy(ref, ref, ks_sem.at[s, half, r], kr_sem.at[s, half, src], r, t)

    for s in range(seqs):
        finish(xg[s])
        for half in range(2):
            rows = xf[s, half * hslots:(half + 1) * hslots].reshape(piece, hid)
            out = mm_nt(rows, wqkv[...])
            kv[s, kv_piece(half)] = out[:, :lanes].astype(BF16)
            for i in range(qh):
                qs[s, half, i * piece:(i + 1) * piece, :] = out[:, lanes * (i + 1):lanes * (i + 2)].astype(BF16)
            for i in range(1, cps):
                r = (c + i) % cps
                if half == 0:
                    kv_copy(s, half, r, c).start()
                else:
                    @pl.when(r < c)
                    def _():
                        kv_copy(s, half, r, c).start()

    scale = hd ** -0.5
    causal = lax.broadcasted_iota(jnp.int32, (piece, piece), 1) <= lax.broadcasted_iota(jnp.int32, (piece, piece), 0)
    lane_lo = lax.broadcasted_iota(jnp.int32, (n, lanes), 1) < hd
    mid = piece // 2

    def attend(s, half):
        blocks = jnp.where(half == 0, c + 1, pieces - c)
        for i in range(qh):
            rs = slice(i * piece, (i + 1) * piece)
            mx[rs] = jnp.full((piece, mid), -jnp.inf, F32)

        def scores(j, diag):
            for i in range(qh):
                rs = slice(i * piece, (i + 1) * piece)
                sc = mm_nt(qs[s, half, rs, :], kv[s, j])
                if diag:
                    sc = jnp.where(causal, sc, -jnp.inf)
                sbuf[j, rs, :] = sc
                mx[rs] = jnp.maximum(mx[rs], jnp.maximum(sc[:, :mid], sc[:, mid:]))

        def one(j, _):
            scores(j, False)
            return 0

        lax.fori_loop(0, blocks - 1, one, 0)
        scores(blocks - 1, True)
        for i in range(qh):
            rs = slice(i * piece, (i + 1) * piece)
            mx[rs] = jnp.broadcast_to(jnp.max(mx[rs], axis=1, keepdims=True), (piece, mid))
            lsum[rs] = jnp.zeros((piece, mid), F32)
            acc[rs] = jnp.zeros((piece, lanes), F32)

        def two(j, _):
            for i in range(qh):
                rs = slice(i * piece, (i + 1) * piece)
                top = mx[rs]
                pa = jnp.exp((sbuf[j, rs, :mid] - top) * scale)
                pb = jnp.exp((sbuf[j, rs, mid:] - top) * scale)
                lsum[rs] += pa + pb
                acc[rs] += mm(jnp.concatenate([pa, pb], axis=1).astype(BF16), kv[s, j])
            return 0

        lax.fori_loop(0, blocks, two, 0)
        for u in range(hslots):
            heads = []
            for i in range(qh):
                rs = slice(i * piece + u * n, i * piece + (u + 1) * n)
                heads.append(acc[rs] / jnp.sum(lsum[rs], axis=1, keepdims=True))
            for b in range(0, qh, 2):
                if b + 1 < qh:
                    both = jnp.where(lane_lo, heads[b], pltpu.roll(heads[b + 1], hd, 1))
                else:
                    both = jnp.where(lane_lo, heads[b], 0.0)
                osend[s, half * hslots + u, :, b * hd:b * hd + lanes] = both.astype(BF16)
        for u in range(hslots):
            dst = half * hslots + u

            @pl.when(dst != t)
            def _():
                rcopy(osend.at[s, dst], orecv.at[s, t], os_sem.at[s, dst], or_sem.at[s, t], c, dst).start()

            @pl.when(dst == t)
            def _():
                orecv[s, t] = osend[s, t]

    for s in range(seqs):
        for i in range(1, cps):
            r = (c + i) % cps
            kv_copy(s, 0, c, r).wait_recv()

            @pl.when(r > c)
            def _():
                kv_copy(s, 1, c, r).wait_recv()

        def half_body(half, _, s=s):
            attend(s, half)
            return 0

        lax.fori_loop(0, 2, half_body, 0)

    relay(wg_parts)
    finish(wg_parts)

    def exchange(src, dst, ss, rs):
        def go(i, _):
            g = (me + i) % group
            rcopy(src.at[g], dst.at[me], ss, rs, g // tps, g % tps).start()
            return 0

        lax.fori_loop(1, group, go, 0)
        dst[me] = src[me]

    def arrived(dst, rs):
        part = dst.at[pl.ds(0, group - 1)]
        rcopy(part, part, rs, rs, c, t).wait_recv()

    def left_all(src, ss):
        part = src.at[pl.ds(0, group - 1)]
        rcopy(part, part, ss, ss, c, t).wait_send()

    for s in range(seqs):
        for i in range(1, tps):
            src = (t + i) % tps
            rcopy(orecv.at[s, src], orecv.at[s, src], os_sem.at[s, src], or_sem.at[s, src], c, src).wait_recv()
        total = xf[s, t].astype(F32)
        added = None
        for u in range(tps):
            term = mm(orecv[s, u][:, :kdim], wof[u])
            added = term if added is None else added + term
        mid_rows = (total + added).astype(BF16)
        hbuf[s] = mid_rows
        dsend[s] = mm(onehot[s], mid_rows).reshape(group, cap, hid).astype(BF16)
        exchange(dsend.at[s], drecv.at[s], ds_sem.at[s], dr_sem.at[s])

    for cp in ld_exp:
        cp.wait()
    for s in range(seqs):
        arrived(drecv.at[s], dr_sem.at[s])
        rows = drecv[s].astype(F32).reshape(group * cap, hid).astype(BF16)
        act = (jax.nn.silu(mm(rows, wg[...])) * mm(rows, wu[...])).astype(BF16)
        rsend[s] = mm(act, wd[...]).reshape(group, cap, hid).astype(BF16)
        exchange(rsend.at[s], rrecv.at[s], rs_sem.at[s], rr_sem.at[s])

    for s in range(seqs):
        arrived(rrecv.at[s], rr_sem.at[s])
        z = mm(onehot_t[s], rrecv[s].astype(F32).reshape(group * cap, hid).astype(BF16))
        g0 = gcol[s, 0][:, :1]
        g1 = gcol[s, 1][:, :1]
        y_ref[s] = (hbuf[s].astype(F32) + (g0 * z[:n] + g1 * z[n:])).astype(BF16)

    for s in range(seqs):
        for k in range(11):
            xg[s][2](k)
        for half in range(2):
            for i in range(1, cps):
                r = (c + i) % cps
                if half == 0:
                    kv_copy(s, half, r, c).wait_send()
                else:
                    @pl.when(r < c)
                    def _():
                        kv_copy(s, half, r, c).wait_send()
        for i in range(1, tps):
            dst = (t + i) % tps
            rcopy(osend.at[s, dst], orecv.at[s, t], os_sem.at[s, dst], or_sem.at[s, t], c, dst).wait_send()
        left_all(dsend.at[s], ds_sem.at[s])
        left_all(rsend.at[s], rs_sem.at[s])
    for k in range(11):
        wg_parts[2](k)


def solution(mesh):
    cps = mesh.shape['cp']
    tps = mesh.shape['tp']
    experts = cps * tps
    row_spec = P(None, ('data', 'cp', 'tp'), None)
    head_spec = P(None, 'tp', None)
    out_spec = P('tp', None, None)
    expert_spec = P(('cp', 'tp'), None, None)

    def device_step(act_in, route_ids, route_gates, w_query, w_key, w_value, w_out, w_gate, w_up, w_down):
        seqs, n, hid = act_in.shape
        qh, hd = w_query.shape[1], w_query.shape[2]
        ff = w_gate.shape[2]
        cap = (4 * n) // experts
        kdim = qh * hd
        lanes = 2 * hd
        hslots = tps // 2
        piece = n * hslots
        wq = jnp.transpose(w_query, (1, 2, 0)).reshape(kdim, hid)
        wk = jnp.transpose(w_key, (1, 2, 0)).reshape(hd, hid)
        wv = jnp.transpose(w_value, (1, 2, 0)).reshape(hd, hid)
        ids = jnp.transpose(route_ids, (0, 2, 1))
        gates = jnp.transpose(route_gates, (0, 2, 1))
        dims = (cps, tps, seqs, n, hid, hd, qh, cap)
        owid = lanes * ((qh + 1) // 2)
        vm = pl.BlockSpec(memory_space=pltpu.VMEM)
        anym = pl.BlockSpec(memory_space=pl.ANY)
        dma = pltpu.SemaphoreType.DMA
        scratch = [
            pltpu.VMEM((seqs, tps, n, hid), BF16),
            pltpu.VMEM((lanes * (qh + 1), hid), BF16),
            pltpu.VMEM((seqs, 2 * cps, piece, lanes), BF16),
            pltpu.VMEM((seqs, 2, qh * piece, lanes), BF16),
            pltpu.VMEM((2 * cps, qh * piece, piece), F32),
            pltpu.VMEM((qh * piece, piece // 2), F32),
            pltpu.VMEM((qh * piece, piece // 2), F32),
            pltpu.VMEM((qh * piece, lanes), F32),
            pltpu.VMEM((seqs, tps, n, owid), BF16),
            pltpu.VMEM((seqs, tps, n, owid), BF16),
            pltpu.VMEM((tps, kdim, hid), BF16),
            pltpu.VMEM((seqs, experts * cap, n), BF16),
            pltpu.VMEM((seqs, 2 * n, experts * cap), BF16),
            pltpu.VMEM((seqs, 2, n, 128), F32),
            pltpu.VMEM((seqs, n, hid), BF16),
            pltpu.VMEM((seqs, experts, cap, hid), BF16),
            pltpu.VMEM((seqs, experts, cap, hid), BF16),
            pltpu.VMEM((seqs, experts, cap, hid), BF16),
            pltpu.VMEM((seqs, experts, cap, hid), BF16),
            pltpu.VMEM((hid, ff), BF16),
            pltpu.VMEM((hid, ff), BF16),
            pltpu.VMEM((ff, hid), BF16),
            dma((8 + qh,)),
            dma((seqs, 11)), dma((seqs, 11)),
            dma((11,)), dma((11,)),
            dma((seqs, 2, cps)), dma((seqs, 2, cps)),
            dma((seqs, tps)), dma((seqs, tps)),
            dma((seqs,)), dma((seqs,)),
            dma((seqs,)), dma((seqs,)),
        ]
        return pl.pallas_call(
            functools.partial(layer_kernel, dims),
            out_shape=jax.ShapeDtypeStruct((seqs, n, hid), BF16),
            in_specs=[anym, vm, vm, anym, anym, anym, anym, anym, anym, anym],
            out_specs=vm,
            scratch_shapes=scratch,
            compiler_params=pltpu.CompilerParams(collective_id=0, has_side_effects=True, vmem_limit_bytes=58 * 1024 * 1024),
            name='layer',
        )(act_in, ids, gates, wq, wk, wv, w_out.reshape(kdim, hid), w_gate[0], w_up[0], w_down[0])

    return jax.shard_map(device_step, mesh=mesh, in_specs=(row_spec, row_spec, row_spec, head_spec, head_spec, head_spec, out_spec, expert_spec, expert_spec, expert_spec), out_specs=row_spec, check_vma=False)
```

time: 233 us -> 101 us (0.43)
  Pallas kernels: 0 us -> 99.1 us
  waiting for transfers between devices: 84.2 us -> 0 us
  blocking collectives: 49.5 us -> 0 us
  matrix products: 34.1 us -> 0 us
  local copies, waits for them, and re-layouts: 32.4 us -> 1.77 us
  other arithmetic: 14.5 us -> 0 us
  between operations: 13.7 us -> 0.01 us
  starting transfers between devices: 4.06 us -> 0 us
    pallas_call x0 -> x1, Pallas kernels: none -> 99.1 us  [device_step(): pl.pallas_call(functools.partial(layer_kernel, dims), out_shape=jax.Shape...]
    dot_general x10 -> x0, matrix products: 34.1 us -> none  [the longest x2 9.76 us: attend_local(): jnp.einsum('bhgqk,bkhd->bqhgd', exp_scores.astype(jnp.bfloat16), value_al...]
    all_gather x1 -> x0, waiting for transfers between devices: 30 us -> none  [attend_local(): x_half = lax.all_gather(act_in, 'tp', axis=1, tiled=True)]
    reduce_scatter x1 -> x0, waiting for transfers between devices: 29.5 us -> none  [attend_local(): attn_sum = lax.psum_scatter(partial, 'tp', scatter_dimension=1, tiled=True)]
    all_to_all x1 -> x0, blocking collectives: 28.2 us -> none  [dispatch_experts(): recv_buf = lax.all_to_all(send_buf, ('cp', 'tp'), 1, 1, tiled=True)]
    all_to_all x1 -> x0, waiting for transfers between devices: 24 us -> none  [dispatch_experts(): lax.all_to_all(expert_out.reshape(n_micro, experts, capacity, hidden), ('...]
    all_gather x2 -> x0, blocking collectives: 21.2 us -> none  [the longest x1 11.3 us: attend_local(): value_all = lax.all_gather(value_half, 'cp', axis=1, tiled=True)]
    gather x3 -> x0, local copies, waits for them, and re-layouts: 13.5 us -> none  [pick_rows(): return jnp.take(row_table, row_ids, axis=0, mode='fill', fill_value=0)]
  transfers between devices with their start and end apart: 3 -> 0, of which waited for: 3 -> 0; matrix products, arithmetic and copies ran while one was open for 7% -> 0% of each run, Pallas kernels for 0% -> 0%
where the time goes in v1:
time: 101 us
  Pallas kernels  99.1 us (98%)
  local copies, waits for them, and re-layouts  1.77 us (2%)
    pallas_call x1, Pallas kernels, device_step(): pl.pallas_call(functools.partial(layer_kernel, dims), out_shape=jax.Shape...  99.1 us

profile of v1, /device:TPU:97, one launch (start us, length us, event | category | flops | bytes accessed | tf_op | source)
XLA Modules:
  0.0 100.9 jit_solution(13852260489221119728)
XLA Ops:
  0.0 99.1 %layer.1 = bf16[2,64,1536]{2,1,0:T(8,128)(2,1)} custom-call(bf16[2,64,1536]{2,1,0:T(8,128)(2,1)} %x_hbm.1, s32[2,2,64]{2,1,0:T(2,128)} %bitcast.22, f32[2,2,64]{2,1,0:T(2,128)} %bitcast.23, bf16[192,1536]{1,0:T(8,128)(2,1)} %bitcast.18, bf16[64,1536]{1,0:T(8,128)(2,1)} %bitcast.20, bf16[64,1536]{1,0:T(8,128)(2,1)} %bitcast.21, bf16[192,1536]{1,0:T(8,128)(2,1)} %bitcast.19, ...), custom_call_target="tpu_custom_call" | custom-call | tf_op jit(solution)/shard_map/layer/pallas_call | solution.py:409
  99.1 1.8 %copy.12 = bf16[2,64,1536]{2,1,0:T(8,128)(2,1)} copy(bf16[2,64,1536]{2,1,0:T(8,128)(2,1)} %layer.1) | data formatting | bytes 786432

commit v2 on v1

--- a/solution.py
+++ b/solution.py
@@ -8,6 +8,7 @@
 from jax.sharding import PartitionSpec as P
 
 MESH = pl.DeviceIdType.MESH
+scope = jax.named_scope
 F32 = jnp.float32
 BF16 = jnp.bfloat16
 NT = (((1,), (1,)), ((), ()))
@@ -24,7 +25,7 @@
 def layer_kernel(dims, x_hbm, ids_ref, gates_ref, wq_hbm, wk_hbm, wv_hbm, wo_hbm, wg_hbm, wu_hbm, wd_hbm, y_ref,
                  xf, wqkv, kv, qs, sbuf, mx, lsum, acc, osend, orecv, wof, onehot, onehot_t, gcol, hbuf,
                  dsend, drecv, rsend, rrecv, wg, wu, wd,
-                 loc_sem, xs_sem, xr_sem, ws_sem, wr_sem, ks_sem, kr_sem, os_sem, or_sem,
+                 loc_sem, xs_sem, xr_sem, ws_sem, wr_sem, vs_sem, vr_sem, ss_sem, sr_sem, ks_sem, kr_sem, os_sem, or_sem,
                  ds_sem, dr_sem, rs_sem, rr_sem):
     cps, tps, seqs, n, hid, hd, qh, cap = dims
     experts = cps * tps
@@ -42,25 +43,28 @@
     xc = t // 2
     core = t % 2
 
+    unit = hid // (cps + 2)
+
     def slot(dx, other):
-        return ((xc + dx) % chips) * 2 + (core if not other else 1 - core)
+        return (xc + dx) % chips, (core if not other else 1 - core)
+
+    def flat(sl):
+        return sl[0] * 2 + sl[1]
 
     right, left, sib = slot(1, False), slot(chips - 1, False), slot(0, True)
+    own, opposite = (xc, core), slot(2, False)
 
     def rcopy(src, dst, ssem, rsem, cc, tt):
         return pltpu.make_async_remote_copy(src_ref=src, dst_ref=dst, send_sem=ssem, recv_sem=rsem,
                                             device_id={'cp': cc, 'tp': tt}, device_id_type=MESH)
 
-    loads = []
-
     def load(src, dst, i):
         cp = pltpu.make_async_copy(src, dst, loc_sem.at[i])
         cp.start()
-        loads.append(cp)
         return cp
 
-    ld_x = [load(x_hbm.at[s], xf.at[s, t], s) for s in range(seqs)]
-    ld_wo = load(wo_hbm, wof.at[t], 2)
+    ld_x = [load(x_hbm.at[s], xf.at[s, xc, core], s) for s in range(seqs)]
+    ld_wo = load(wo_hbm, wof.at[xc, core], 2)
     ld_qkv = [load(wv_hbm, wqkv.at[pl.ds(0, hd)], 3), load(wk_hbm, wqkv.at[pl.ds(hd, hd)], 4)]
     for i in range(qh):
         ld_qkv.append(load(wq_hbm.at[pl.ds(i * hd, hd)], wqkv.at[pl.ds(lanes * (i + 1) + hd, hd)], 5 + i))
@@ -76,51 +80,86 @@
     lax.fori_loop(1, group, sig, 0)
     pl.semaphore_wait(barrier, group - 1)
 
-    def gather_parts(buf, rows, ss, rs, chunked):
-        half = rows // 2
-        lo, hi = pl.ds(0, half), pl.ds(half, half)
-
-        def ref(sl, part):
-            return buf.at[sl] if part is None else buf.at[sl, part]
-
-        def cp(src_slot, part, kind, dst):
-            return rcopy(ref(src_slot, part), ref(src_slot, part), ss.at[kind], rs.at[kind], c, dst)
-
-        nl, nr, op = slot(chips - 1, False), slot(1, False), slot(2, False)
-        snl, snr, sop = slot(chips - 1, True), slot(1, True), slot(2, True)
-        own = t
+    def gather(get, ss, rs):
+        l2, r2, o2 = slot(chips - 1, True), slot(1, True), slot(2, True)
         sends = [
-            (own, lo, right), (own, hi, right), (own, hi, left), (own, lo, left),
-            (nl, lo, right), (nr, hi, left),
-            (own, None, sib), (nl, None, sib), (nr, None, sib), (op, lo, sib), (op, hi, sib),
+            (own, 'lo', right), (own, 'hi', right), (own, 'hi', left), (own, 'lo', left),
+            (left, 'lo', right), (right, 'hi', left),
+            (own, 'all', sib), (left, 'all', sib), (right, 'all', sib), (opposite, 'lo', sib), (opposite, 'hi', sib),
         ]
         gets = [
-            (nl, lo), (nl, hi), (nr, hi), (nr, lo),
-            (op, lo), (op, hi),
-            (sib, None), (snl, None), (snr, None), (sop, lo), (sop, hi),
+            (left, 'lo'), (left, 'hi'), (right, 'hi'), (right, 'lo'),
+            (opposite, 'lo'), (opposite, 'hi'),
+            (sib, 'all'), (l2, 'all'), (r2, 'all'), (o2, 'lo'), (o2, 'hi'),
         ]
 
-        def start(k):
-            s_, p_, d_ = sends[k]
-            cp(s_, p_, k, d_).start()
-
-        def got(k):
-            s_, p_ = gets[k]
-            cp(s_, p_, k, sib).wait_recv()
-
-        def sent(k):
-            s_, p_, d_ = sends[k]
-            cp(s_, p_, k, d_).wait_send()
+        def copy(sl, part, kind, dst):
+            return rcopy(get(sl, part), get(sl, part), ss.at[kind], rs.at[kind], c, flat(dst))
+
+        def start(*kinds):
+            for k in kinds:
+                copy(*sends[k][:2], k, sends[k][2]).start()
+
+        def got(*kinds):
+            for k in kinds:
+                copy(*gets[k], k, sib).wait_recv()
+
+        def sent(*kinds):
+            for k in kinds:
+                copy(*sends[k][:2], k, sends[k][2]).wait_send()
 
         return start, got, sent
 
-    xg = [gather_parts(xf.at[s], n, xs_sem.at[s], xr_sem.at[s], False) for s in range(seqs)]
-    wg_parts = gather_parts(wof, kdim, ws_sem, wr_sem, True)
-
-    for s in range(seqs):
-        ld_x[s].wait()
-        for k in (0, 2, 1, 3, 6):
-            xg[s][0](k)
+    def rows_of(rows):
+        return {'lo': pl.ds(0, rows // 2), 'hi': pl.ds(rows // 2, rows // 2), 'all': pl.ds(0, rows)}
+
+    xparts, wparts = rows_of(n), rows_of(kdim)
+    xg = [gather(lambda sl, part, s=s: xf.at[s, sl[0], sl[1], xparts[part]], xs_sem.at[s], xr_sem.at[s]) for s in range(seqs)]
+
+    cols_a = pl.ds(0, 2 * unit)
+
+    def cols_b(r):
+        return pl.ds(pl.multiple_of((r + 2) * unit, unit), unit)
+
+    wa = gather(lambda sl, part: wof.at[sl[0], sl[1], wparts[part], cols_a], ws_sem.at[0], wr_sem.at[0])
+    wb = gather(lambda sl, part: wof.at[sl[0], sl[1], wparts[part], cols_b(c)], ws_sem.at[1], wr_sem.at[1])
+    up, down, across = (c + 1) % cps, (c + cps - 1) % cps, (c + 2) % cps
+
+    def spread(q, sl):
+        sends = [(c, 'lo', up), (c, 'hi', up), (c, 'hi', down), (c, 'lo', down), (down, 'lo', up), (up, 'hi', down)]
+        gets = [(down, 'lo'), (down, 'hi'), (up, 'hi'), (up, 'lo'), (across, 'lo'), (across, 'hi')]
+
+        def copy(r, part, kind, dst):
+            ref = wof.at[sl[0], sl[1], wparts[part], cols_b(r)]
+            return rcopy(ref, ref, vs_sem.at[q, kind], vr_sem.at[q, kind], dst, t)
+
+        def start(*kinds):
+            for k in kinds:
+                copy(*sends[k][:2], k, sends[k][2]).start()
+
+        def got(*kinds):
+            for k in kinds:
+                copy(*gets[k], k, up).wait_recv()
+
+        def sent(*kinds):
+            for k in kinds:
+                copy(*sends[k][:2], k, sends[k][2]).wait_send()
+
+        return start, got, sent
+
+    wy = [spread(q, sl) for q, sl in enumerate((left, right, opposite))]
+
+    def share(b, mine):
+        cr = core if mine else 1 - core
+        blk = cols_a if b is None else cols_b(b)
+        ref = wof.at[:, cr, :, blk]
+        k = cps if b is None else b
+        return rcopy(ref, ref, ss_sem.at[k], sr_sem.at[k], c, flat(sib))
+
+    ld_x[0].wait()
+    xg[0][0](0, 2, 1, 3, 6)
+    ld_x[1].wait()
+    xg[1][0](0, 2)
 
     ecol = lax.broadcasted_iota(jnp.int32, (experts, n), 0)
     later = (lax.broadcasted_iota(jnp.int32, (n, n), 0) < lax.broadcasted_iota(jnp.int32, (n, n), 1)).astype(F32).astype(BF16)
@@ -144,34 +183,6 @@
     for i in range(qh):
         wqkv[lanes * (i + 1):lanes * (i + 1) + hd, :] = jnp.zeros((hd, hid), BF16)
 
-    def relay(parts):
-        start, got, sent = parts
-        got(0)
-        start(4)
-        got(2)
-        start(5)
-        got(1)
-        start(7)
-        got(3)
-        start(8)
-
-    def finish(parts):
-        start, got, sent = parts
-        got(4)
-        start(9)
-        got(5)
-        start(10)
-        for k in (6, 7, 8, 9, 10):
-            got(k)
-
-    for s in range(seqs):
-        relay(xg[s])
-    ld_wo.wait()
-    for k in (0, 2, 1, 3, 6):
-        wg_parts[0](k)
-    for cp in ld_qkv:
-        cp.wait()
-
     def kv_piece(half):
         return c if half == 0 else pieces - 1 - c
 
@@ -179,10 +190,9 @@
         ref = kv.at[s, src if half == 0 else pieces - 1 - src]
         return rcopy(ref, ref, ks_sem.at[s, half, r], kr_sem.at[s, half, src], r, t)
 
-    for s in range(seqs):
-        finish(xg[s])
+    def project(s):
         for half in range(2):
-            rows = xf[s, half * hslots:(half + 1) * hslots].reshape(piece, hid)
+            rows = xf[s, half * (chips // 2):(half + 1) * (chips // 2)].reshape(piece, hid)
             out = mm_nt(rows, wqkv[...])
             kv[s, kv_piece(half)] = out[:, :lanes].astype(BF16)
             for i in range(qh):
@@ -196,13 +206,57 @@
                     def _():
                         kv_copy(s, half, r, c).start()
 
+    with scope('xrelay0'):
+        start, got, _ = xg[0]
+        got(0)
+        start(4)
+        got(2)
+        start(5)
+        xg[1][0](1, 3, 6)
+        got(1)
+        start(7)
+        got(3)
+        start(8)
+    with scope('xrelay1'):
+        xg[1][1](0)
+        xg[1][0](4)
+        xg[1][1](2)
+        xg[1][0](5)
+    with scope('xfinish0'):
+        start, got, _ = xg[0]
+        got(4)
+        start(9)
+        got(5)
+        start(10)
+        for cp in ld_qkv:
+            cp.wait()
+        ld_wo.wait()
+        wb[0](0, 2, 1, 3)
+        wa[0](0, 2, 1, 3)
+        got(6, 7, 8, 9, 10)
+    with scope('qkv0'):
+        project(0)
+    with scope('xfinish1'):
+        start, got, _ = xg[1]
+        got(1)
+        start(7)
+        got(3)
+        start(8)
+        got(4)
+        start(9)
+        got(5)
+        start(10)
+        got(6, 7, 8, 9, 10)
+    with scope('qkv1'):
+        project(1)
+
     scale = hd ** -0.5
     causal = lax.broadcasted_iota(jnp.int32, (piece, piece), 1) <= lax.broadcasted_iota(jnp.int32, (piece, piece), 0)
     lane_lo = lax.broadcasted_iota(jnp.int32, (n, lanes), 1) < hd
     mid = piece // 2
 
     def attend(s, half):
-        blocks = jnp.where(half == 0, c + 1, pieces - c)
+        blocks = c + 1 if half == 0 else pieces - c
         for i in range(qh):
             rs = slice(i * piece, (i + 1) * piece)
             mx[rs] = jnp.full((piece, mid), -jnp.inf, F32)
@@ -259,9 +313,9 @@
 
             @pl.when(dst == t)
             def _():
-                orecv[s, t] = osend[s, t]
-
-    for s in range(seqs):
+                orecv[s, t] = osend[s, dst]
+
+    def kv_wait(s):
         for i in range(1, cps):
             r = (c + i) % cps
             kv_copy(s, 0, c, r).wait_recv()
@@ -269,15 +323,6 @@
             @pl.when(r > c)
             def _():
                 kv_copy(s, 1, c, r).wait_recv()
-
-        def half_body(half, _, s=s):
-            attend(s, half)
-            return 0
-
-        lax.fori_loop(0, 2, half_body, 0)
-
-    relay(wg_parts)
-    finish(wg_parts)
 
     def exchange(src, dst, ss, rs):
         def go(i, _):
@@ -296,39 +341,97 @@
         part = src.at[pl.ds(0, group - 1)]
         rcopy(part, part, ss, ss, c, t).wait_send()
 
-    for s in range(seqs):
+    def out_rows(s):
         for i in range(1, tps):
             src = (t + i) % tps
             rcopy(orecv.at[s, src], orecv.at[s, src], os_sem.at[s, src], or_sem.at[s, src], c, src).wait_recv()
-        total = xf[s, t].astype(F32)
+        total = xf[s, xc, core].astype(F32)
         added = None
         for u in range(tps):
-            term = mm(orecv[s, u][:, :kdim], wof[u])
+            term = mm(orecv[s, u][:, :kdim], wof[u // 2, u % 2])
             added = term if added is None else added + term
         mid_rows = (total + added).astype(BF16)
         hbuf[s] = mid_rows
         dsend[s] = mm(onehot[s], mid_rows).reshape(group, cap, hid).astype(BF16)
         exchange(dsend.at[s], drecv.at[s], ds_sem.at[s], dr_sem.at[s])
 
+    with scope('wb1'):
+        wb[1](0)
+        wb[0](4)
+        wb[1](2)
+        wb[0](5)
+        wb[1](1, 3)
+        wy[0][0](0, 2, 1, 3)
+        wy[1][0](0, 2, 1, 3)
+    with scope('kvwait0'):
+        kv_wait(0)
+    with scope('attend01'):
+        attend(0, 1)
+    with scope('wb2'):
+        wb[1](4, 5)
+        wy[2][0](0, 2, 1, 3)
+        share(c, True).start()
+        wa[1](0)
+        wa[0](4)
+        wa[1](2)
+        wa[0](5)
+        wa[1](1, 3)
+    with scope('attend00'):
+        attend(0, 0)
+    with scope('wy1'):
+        for q in range(2):
+            wy[q][1](0)
+            wy[q][0](4)
+            wy[q][1](2)
+            wy[q][0](5)
+            wy[q][1](1, 3)
+    with scope('kvwait1'):
+        kv_wait(1)
+    with scope('attend11'):
+        attend(1, 1)
+    with scope('wy2'):
+        wy[2][1](0)
+        wy[2][0](4)
+        wy[2][1](2)
+        wy[2][0](5)
+        wa[1](4, 5)
+        share(None, True).start()
+        wy[2][1](1, 3)
+        share(down, True).start()
+        share(up, True).start()
+        for q in range(3):
+            wy[q][1](4, 5)
+        share(across, True).start()
+    with scope('wshare'):
+        for b in (c, None, down, up, across):
+            share(b, False).wait_recv()
+    with scope('out0'):
+        out_rows(0)
+    with scope('attend10'):
+        attend(1, 0)
+    with scope('out1'):
+        out_rows(1)
+
     for cp in ld_exp:
         cp.wait()
     for s in range(seqs):
-        arrived(drecv.at[s], dr_sem.at[s])
+        with scope(f'dwait{s}'):
+            arrived(drecv.at[s], dr_sem.at[s])
         rows = drecv[s].astype(F32).reshape(group * cap, hid).astype(BF16)
         act = (jax.nn.silu(mm(rows, wg[...])) * mm(rows, wu[...])).astype(BF16)
         rsend[s] = mm(act, wd[...]).reshape(group, cap, hid).astype(BF16)
         exchange(rsend.at[s], rrecv.at[s], rs_sem.at[s], rr_sem.at[s])
 
     for s in range(seqs):
-        arrived(rrecv.at[s], rr_sem.at[s])
+        with scope(f'rwait{s}'):
+            arrived(rrecv.at[s], rr_sem.at[s])
         z = mm(onehot_t[s], rrecv[s].astype(F32).reshape(group * cap, hid).astype(BF16))
         g0 = gcol[s, 0][:, :1]
         g1 = gcol[s, 1][:, :1]
         y_ref[s] = (hbuf[s].astype(F32) + (g0 * z[:n] + g1 * z[n:])).astype(BF16)
 
     for s in range(seqs):
-        for k in range(11):
-            xg[s][2](k)
+        xg[s][2](*range(11))
         for half in range(2):
             for i in range(1, cps):
                 r = (c + i) % cps
@@ -343,8 +446,10 @@
             rcopy(osend.at[s, dst], orecv.at[s, t], os_sem.at[s, dst], or_sem.at[s, t], c, dst).wait_send()
         left_all(dsend.at[s], ds_sem.at[s])
         left_all(rsend.at[s], rs_sem.at[s])
-    for k in range(11):
-        wg_parts[2](k)
+    for part in (wa, wb, *wy):
+        part[2](*range(6))
+    for b in (c, None, down, up, across):
+        share(b, True).wait_send()
 
 
 def solution(mesh):
@@ -376,7 +481,7 @@
         anym = pl.BlockSpec(memory_space=pl.ANY)
         dma = pltpu.SemaphoreType.DMA
         scratch = [
-            pltpu.VMEM((seqs, tps, n, hid), BF16),
+            pltpu.VMEM((seqs, tps // 2, 2, n, hid), BF16),
             pltpu.VMEM((lanes * (qh + 1), hid), BF16),
             pltpu.VMEM((seqs, 2 * cps, piece, lanes), BF16),
             pltpu.VMEM((seqs, 2, qh * piece, lanes), BF16),
@@ -386,7 +491,7 @@
             pltpu.VMEM((qh * piece, lanes), F32),
             pltpu.VMEM((seqs, tps, n, owid), BF16),
             pltpu.VMEM((seqs, tps, n, owid), BF16),
-            pltpu.VMEM((tps, kdim, hid), BF16),
+            pltpu.VMEM((tps // 2, 2, kdim, hid), BF16),
             pltpu.VMEM((seqs, experts * cap, n), BF16),
             pltpu.VMEM((seqs, 2 * n, experts * cap), BF16),
             pltpu.VMEM((seqs, 2, n, 128), F32),
@@ -400,7 +505,9 @@
             pltpu.VMEM((ff, hid), BF16),
             dma((8 + qh,)),
             dma((seqs, 11)), dma((seqs, 11)),
-            dma((11,)), dma((11,)),
+            dma((2, 6)), dma((2, 6)),
+            dma((3, 6)), dma((3, 6)),
+            dma((cps + 1,)), dma((cps + 1,)),
             dma((seqs, 2, cps)), dma((seqs, 2, cps)),
             dma((seqs, tps)), dma((seqs, tps)),
             dma((seqs,)), dma((seqs,)),

time: 101 us -> 103 us (1.020); the launches traced: 101 us -> 102 us
  no operation moved by 1% of the time
where the time goes in v2:
time: 103 us; the launch traced here: 102 us
  Pallas kernels  99.9 us (97%)
  local copies, waits for them, and re-layouts  1.77 us (2%)
    pallas_call x1, Pallas kernels, device_step(): pl.pallas_call(functools.partial(layer_kernel, dims), out_shape=jax.Shape...  99.9 us

profile of v2, /device:TPU:97, one launch (start us, length us, event | category | flops | bytes accessed | tf_op | source)
XLA Modules:
  0.0 101.6 jit_solution(8465483002168016075)
XLA Ops:
  0.0 99.9 %layer.1 = bf16[2,64,1536]{2,1,0:T(8,128)(2,1)} custom-call(bf16[2,64,1536]{2,1,0:T(8,128)(2,1)} %x_hbm.1, s32[2,2,64]{2,1,0:T(2,128)} %bitcast.22, f32[2,2,64]{2,1,0:T(2,128)} %bitcast.23, bf16[192,1536]{1,0:T(8,128)(2,1)} %bitcast.18, bf16[64,1536]{1,0:T(8,128)(2,1)} %bitcast.20, bf16[64,1536]{1,0:T(8,128)(2,1)} %bitcast.21, bf16[192,1536]{1,0:T(8,128)(2,1)} %bitcast.19, ...), custom_call_target="tpu_custom_call" | custom-call | tf_op jit(solution)/shard_map/layer/pallas_call | solution.py:516
  99.9 1.8 %copy.12 = bf16[2,64,1536]{2,1,0:T(8,128)(2,1)} copy(bf16[2,64,1536]{2,1,0:T(8,128)(2,1)} %layer.1) | data formatting | bytes 786432

commit v3 on v2

--- a/solution.py
+++ b/solution.py
@@ -43,7 +43,7 @@
     xc = t // 2
     core = t % 2
 
-    unit = hid // (cps + 2)
+    unit = hid // (3 * cps)
 
     def slot(dx, other):
         return (xc + dx) % chips, (core if not other else 1 - core)
@@ -116,10 +116,10 @@
     xparts, wparts = rows_of(n), rows_of(kdim)
     xg = [gather(lambda sl, part, s=s: xf.at[s, sl[0], sl[1], xparts[part]], xs_sem.at[s], xr_sem.at[s]) for s in range(seqs)]
 
-    cols_a = pl.ds(0, 2 * unit)
+    cols_a = pl.ds(0, hid - cps * unit)
 
     def cols_b(r):
-        return pl.ds(pl.multiple_of((r + 2) * unit, unit), unit)
+        return pl.ds(pl.multiple_of(hid - cps * unit + r * unit, unit), unit)
 
     wa = gather(lambda sl, part: wof.at[sl[0], sl[1], wparts[part], cols_a], ws_sem.at[0], wr_sem.at[0])
     wb = gather(lambda sl, part: wof.at[sl[0], sl[1], wparts[part], cols_b(c)], ws_sem.at[1], wr_sem.at[1])
@@ -399,6 +399,9 @@
         wy[2][1](1, 3)
         share(down, True).start()
         share(up, True).start()
+    with scope('attend10'):
+        attend(1, 0)
+    with scope('wy3'):
         for q in range(3):
             wy[q][1](4, 5)
         share(across, True).start()
@@ -407,8 +410,6 @@
             share(b, False).wait_recv()
     with scope('out0'):
         out_rows(0)
-    with scope('attend10'):
-        attend(1, 0)
     with scope('out1'):
         out_rows(1)
 

time: 103 us -> 94 us (0.913); the launches traced: 102 us -> 93.9 us
  Pallas kernels: 99.9 us -> 92.1 us
    pallas_call x1, Pallas kernels: 99.9 us -> 92.1 us  [device_step(): pl.pallas_call(functools.partial(layer_kernel, dims), out_shape=jax.Shape...]
where the time goes in v3:
time: 94 us; the launch traced here: 93.9 us
  Pallas kernels  92.1 us (98%)
  local copies, waits for them, and re-layouts  1.77 us (2%)
    pallas_call x1, Pallas kernels, device_step(): pl.pallas_call(functools.partial(layer_kernel, dims), out_shape=jax.Shape...  92.1 us

profile of v3, /device:TPU:97, one launch (start us, length us, event | category | flops | bytes accessed | tf_op | source)
XLA Modules:
  0.0 93.9 jit_solution(12664094734471536287)
XLA Ops:
  0.0 92.1 %layer.1 = bf16[2,64,1536]{2,1,0:T(8,128)(2,1)} custom-call(bf16[2,64,1536]{2,1,0:T(8,128)(2,1)} %x_hbm.1, s32[2,2,64]{2,1,0:T(2,128)} %bitcast.22, f32[2,2,64]{2,1,0:T(2,128)} %bitcast.23, bf16[192,1536]{1,0:T(8,128)(2,1)} %bitcast.18, bf16[64,1536]{1,0:T(8,128)(2,1)} %bitcast.20, bf16[64,1536]{1,0:T(8,128)(2,1)} %bitcast.21, bf16[192,1536]{1,0:T(8,128)(2,1)} %bitcast.19, ...), custom_call_target="tpu_custom_call" | custom-call | tf_op jit(solution)/shard_map/layer/pallas_call | solution.py:517
  92.1 1.8 %copy.12 = bf16[2,64,1536]{2,1,0:T(8,128)(2,1)} copy(bf16[2,64,1536]{2,1,0:T(8,128)(2,1)} %layer.1) | data formatting | bytes 786432

commit v4 on v3

--- a/solution.py
+++ b/solution.py
@@ -123,38 +123,27 @@
 
     wa = gather(lambda sl, part: wof.at[sl[0], sl[1], wparts[part], cols_a], ws_sem.at[0], wr_sem.at[0])
     wb = gather(lambda sl, part: wof.at[sl[0], sl[1], wparts[part], cols_b(c)], ws_sem.at[1], wr_sem.at[1])
-    up, down, across = (c + 1) % cps, (c + cps - 1) % cps, (c + 2) % cps
-
-    def spread(q, sl):
-        sends = [(c, 'lo', up), (c, 'hi', up), (c, 'hi', down), (c, 'lo', down), (down, 'lo', up), (up, 'hi', down)]
-        gets = [(down, 'lo'), (down, 'hi'), (up, 'hi'), (up, 'lo'), (across, 'lo'), (across, 'hi')]
-
-        def copy(r, part, kind, dst):
-            ref = wof.at[sl[0], sl[1], wparts[part], cols_b(r)]
-            return rcopy(ref, ref, vs_sem.at[q, kind], vr_sem.at[q, kind], dst, t)
-
-        def start(*kinds):
-            for k in kinds:
-                copy(*sends[k][:2], k, sends[k][2]).start()
-
-        def got(*kinds):
-            for k in kinds:
-                copy(*gets[k], k, up).wait_recv()
-
-        def sent(*kinds):
-            for k in kinds:
-                copy(*sends[k][:2], k, sends[k][2]).wait_send()
-
-        return start, got, sent
-
-    wy = [spread(q, sl) for q, sl in enumerate((left, right, opposite))]
-
-    def share(b, mine):
+
+    remote = (left, right, opposite)
+
+    def spread(q, r, src):
+        sl = remote[q]
+        ref = wof.at[sl[0], sl[1], :, cols_b(src)]
+        return rcopy(ref, ref, vs_sem.at[q, r], vr_sem.at[q, src], r, t)
+
+    def share(k, mine):
         cr = core if mine else 1 - core
-        blk = cols_a if b is None else cols_b(b)
-        ref = wof.at[:, cr, :, blk]
-        k = cps if b is None else b
+        if k == 0:
+            ref = wof.at[xc, cr]
+        elif k < 5:
+            q, part = ((0, 'all'), (1, 'all'), (2, 'lo'), (2, 'hi'))[k - 1]
+            ref = wof.at[remote[q][0], cr, wparts[part], cols_a]
+        else:
+            q, i = (k - 5) % 3, (k - 5) // 3
+            ref = wof.at[remote[q][0], cr, :, cols_b((c + i) % cps)]
         return rcopy(ref, ref, ss_sem.at[k], sr_sem.at[k], c, flat(sib))
+
+    shares = 5 + 3 * cps
 
     ld_x[0].wait()
     xg[0][0](0, 2, 1, 3, 6)
@@ -233,6 +222,7 @@
         ld_wo.wait()
         wb[0](0, 2, 1, 3)
         wa[0](0, 2, 1, 3)
+        share(0, True).start()
         got(6, 7, 8, 9, 10)
     with scope('qkv0'):
         project(0)
@@ -315,14 +305,18 @@
             def _():
                 orecv[s, t] = osend[s, dst]
 
-    def kv_wait(s):
+    def kv_wait(s, half):
         for i in range(1, cps):
             r = (c + i) % cps
-            kv_copy(s, 0, c, r).wait_recv()
-
-            @pl.when(r > c)
-            def _():
-                kv_copy(s, 1, c, r).wait_recv()
+            if half == 0:
+                @pl.when(r < c)
+                def _():
+                    kv_copy(s, 0, c, r).wait_recv()
+            else:
+                @pl.when(r > c)
+                def _():
+                    kv_copy(s, 0, c, r).wait_recv()
+                    kv_copy(s, 1, c, r).wait_recv()
 
     def exchange(src, dst, ss, rs):
         def go(i, _):
@@ -361,53 +355,52 @@
         wb[1](2)
         wb[0](5)
         wb[1](1, 3)
-        wy[0][0](0, 2, 1, 3)
-        wy[1][0](0, 2, 1, 3)
-    with scope('kvwait0'):
-        kv_wait(0)
-    with scope('attend01'):
-        attend(0, 1)
+        for q in range(2):
+            for i in range(1, cps):
+                spread(q, (c + i) % cps, c).start()
+    with scope('kvwait00'):
+        kv_wait(0, 0)
+    with scope('attend00'):
+        attend(0, 0)
     with scope('wb2'):
         wb[1](4, 5)
-        wy[2][0](0, 2, 1, 3)
-        share(c, True).start()
+        for i in range(1, cps):
+            spread(2, (c + i) % cps, c).start()
+        for k in (5, 6, 7):
+            share(k, True).start()
         wa[1](0)
         wa[0](4)
         wa[1](2)
         wa[0](5)
+    with scope('kvwait01'):
+        kv_wait(0, 1)
+    with scope('attend01'):
+        attend(0, 1)
+    with scope('wa2'):
         wa[1](1, 3)
-    with scope('attend00'):
-        attend(0, 0)
-    with scope('wy1'):
-        for q in range(2):
-            wy[q][1](0)
-            wy[q][0](4)
-            wy[q][1](2)
-            wy[q][0](5)
-            wy[q][1](1, 3)
-    with scope('kvwait1'):
-        kv_wait(1)
+        share(1, True).start()
+        share(2, True).start()
+    with scope('kvwait10'):
+        kv_wait(1, 0)
+    with scope('attend10'):
+        attend(1, 0)
+    with scope('kvwait11'):
+        kv_wait(1, 1)
     with scope('attend11'):
         attend(1, 1)
-    with scope('wy2'):
-        wy[2][1](0)
-        wy[2][0](4)
-        wy[2][1](2)
-        wy[2][0](5)
-        wa[1](4, 5)
-        share(None, True).start()
-        wy[2][1](1, 3)
-        share(down, True).start()
-        share(up, True).start()
-    with scope('attend10'):
-        attend(1, 0)
-    with scope('wy3'):
+    with scope('wa3'):
+        wa[1](4)
+        share(3, True).start()
+        wa[1](5)
+        share(4, True).start()
+    with scope('wy'):
         for q in range(3):
-            wy[q][1](4, 5)
-        share(across, True).start()
+            for i in range(1, cps):
+                spread(q, (c + i) % cps, (c + i) % cps).wait_recv()
+                share(5 + 3 * i + q, True).start()
     with scope('wshare'):
-        for b in (c, None, down, up, across):
-            share(b, False).wait_recv()
+        for k in range(shares):
+            share(k, False).wait_recv()
     with scope('out0'):
         out_rows(0)
     with scope('out1'):
@@ -447,10 +440,13 @@
             rcopy(osend.at[s, dst], orecv.at[s, t], os_sem.at[s, dst], or_sem.at[s, t], c, dst).wait_send()
         left_all(dsend.at[s], ds_sem.at[s])
         left_all(rsend.at[s], rs_sem.at[s])
-    for part in (wa, wb, *wy):
+    for part in (wa, wb):
         part[2](*range(6))
-    for b in (c, None, down, up, across):
-        share(b, True).wait_send()
+    for q in range(3):
+        for i in range(1, cps):
+            spread(q, (c + i) % cps, c).wait_send()
+    for k in range(shares):
+        share(k, True).wait_send()
 
 
 def solution(mesh):
@@ -507,8 +503,8 @@
             dma((8 + qh,)),
             dma((seqs, 11)), dma((seqs, 11)),
             dma((2, 6)), dma((2, 6)),
-            dma((3, 6)), dma((3, 6)),
-            dma((cps + 1,)), dma((cps + 1,)),
+            dma((3, cps)), dma((3, cps)),
+            dma((5 + 3 * cps,)), dma((5 + 3 * cps,)),
             dma((seqs, 2, cps)), dma((seqs, 2, cps)),
             dma((seqs, tps)), dma((seqs, tps)),
             dma((seqs,)), dma((seqs,)),

time: 94 us -> 94.1 us (level)
  no operation moved by 1% of the time
where the time goes in v4:
time: 94.1 us; the launch traced here: 94 us
  Pallas kernels  92.2 us (98%)
  local copies, waits for them, and re-layouts  1.77 us (2%)
    pallas_call x1, Pallas kernels, device_step(): pl.pallas_call(functools.partial(layer_kernel, dims), out_shape=jax.Shape...  92.2 us

profile of v4, /device:TPU:97, one launch (start us, length us, event | category | flops | bytes accessed | tf_op | source)
XLA Modules:
  0.0 94.0 jit_solution(2736351922127124061)
XLA Ops:
  0.0 92.2 %layer.1 = bf16[2,64,1536]{2,1,0:T(8,128)(2,1)} custom-call(bf16[2,64,1536]{2,1,0:T(8,128)(2,1)} %x_hbm.1, s32[2,2,64]{2,1,0:T(2,128)} %bitcast.22, f32[2,2,64]{2,1,0:T(2,128)} %bitcast.23, bf16[192,1536]{1,0:T(8,128)(2,1)} %bitcast.18, bf16[64,1536]{1,0:T(8,128)(2,1)} %bitcast.20, bf16[64,1536]{1,0:T(8,128)(2,1)} %bitcast.21, bf16[192,1536]{1,0:T(8,128)(2,1)} %bitcast.19, ...), custom_call_target="tpu_custom_call" | custom-call | tf_op jit(solution)/shard_map/layer/pallas_call | solution.py:513
  92.2 1.8 %copy.12 = bf16[2,64,1536]{2,1,0:T(8,128)(2,1)} copy(bf16[2,64,1536]{2,1,0:T(8,128)(2,1)} %layer.1) | data formatting | bytes 786432

commit v5 on v4

--- a/solution.py
+++ b/solution.py
@@ -22,8 +22,8 @@
     return lax.dot_general(a, b, NT, preferred_element_type=F32)
 
 
-def layer_kernel(dims, x_hbm, ids_ref, gates_ref, wq_hbm, wk_hbm, wv_hbm, wo_hbm, wg_hbm, wu_hbm, wd_hbm, y_ref,
-                 xf, wqkv, kv, qs, sbuf, mx, lsum, acc, osend, orecv, wof, onehot, onehot_t, gcol, hbuf,
+def layer_kernel(dims, x_hbm, ids_ref, gates_ref, wq_hbm, wk_hbm, wv_hbm, wo_hbm, wg_hbm, wu_hbm, wd_hbm, h_out, w_out,
+                 xf, wqkv, kv, qs, sbuf, mx, lsum, acc, osend, orecv, wof, onehot, onehot_t, gcol, hbuf, wbuf,
                  dsend, drecv, rsend, rrecv, wg, wu, wd,
                  loc_sem, xs_sem, xr_sem, ws_sem, wr_sem, vs_sem, vr_sem, ss_sem, sr_sem, ks_sem, kr_sem, os_sem, or_sem,
                  ds_sem, dr_sem, rs_sem, rr_sem):
@@ -346,6 +346,7 @@
             added = term if added is None else added + term
         mid_rows = (total + added).astype(BF16)
         hbuf[s] = mid_rows
+        pltpu.make_async_copy(hbuf.at[s], h_out.at[s], loc_sem.at[s]).start()
         dsend[s] = mm(onehot[s], mid_rows).reshape(group, cap, hid).astype(BF16)
         exchange(dsend.at[s], drecv.at[s], ds_sem.at[s], dr_sem.at[s])
 
@@ -368,15 +369,15 @@
             spread(2, (c + i) % cps, c).start()
         for k in (5, 6, 7):
             share(k, True).start()
-        wa[1](0)
-        wa[0](4)
-        wa[1](2)
-        wa[0](5)
     with scope('kvwait01'):
         kv_wait(0, 1)
     with scope('attend01'):
         attend(0, 1)
     with scope('wa2'):
+        wa[1](0)
+        wa[0](4)
+        wa[1](2)
+        wa[0](5)
         wa[1](1, 3)
         share(1, True).start()
         share(2, True).start()
@@ -422,9 +423,12 @@
         z = mm(onehot_t[s], rrecv[s].astype(F32).reshape(group * cap, hid).astype(BF16))
         g0 = gcol[s, 0][:, :1]
         g1 = gcol[s, 1][:, :1]
-        y_ref[s] = (hbuf[s].astype(F32) + (g0 * z[:n] + g1 * z[n:])).astype(BF16)
+        wbuf[s] = g0 * z[:n] + g1 * z[n:]
+        pltpu.make_async_copy(wbuf.at[s], w_out.at[s], loc_sem.at[2 + s]).start()
 
     for s in range(seqs):
+        pltpu.make_async_copy(hbuf.at[s], h_out.at[s], loc_sem.at[s]).wait()
+        pltpu.make_async_copy(wbuf.at[s], w_out.at[s], loc_sem.at[2 + s]).wait()
         xg[s][2](*range(11))
         for half in range(2):
             for i in range(1, cps):
@@ -493,6 +497,7 @@
             pltpu.VMEM((seqs, 2 * n, experts * cap), BF16),
             pltpu.VMEM((seqs, 2, n, 128), F32),
             pltpu.VMEM((seqs, n, hid), BF16),
+            pltpu.VMEM((seqs, n, hid), F32),
             pltpu.VMEM((seqs, experts, cap, hid), BF16),
             pltpu.VMEM((seqs, experts, cap, hid), BF16),
             pltpu.VMEM((seqs, experts, cap, hid), BF16),
@@ -510,14 +515,15 @@
             dma((seqs,)), dma((seqs,)),
             dma((seqs,)), dma((seqs,)),
         ]
-        return pl.pallas_call(
+        mid, added = pl.pallas_call(
             functools.partial(layer_kernel, dims),
-            out_shape=jax.ShapeDtypeStruct((seqs, n, hid), BF16),
+            out_shape=[jax.ShapeDtypeStruct((seqs, n, hid), BF16), jax.ShapeDtypeStruct((seqs, n, hid), F32)],
             in_specs=[anym, vm, vm, anym, anym, anym, anym, anym, anym, anym],
-            out_specs=vm,
+            out_specs=[anym, anym],
             scratch_shapes=scratch,
             compiler_params=pltpu.CompilerParams(collective_id=0, has_side_effects=True, vmem_limit_bytes=58 * 1024 * 1024),
             name='layer',
         )(act_in, ids, gates, wq, wk, wv, w_out.reshape(kdim, hid), w_gate[0], w_up[0], w_down[0])
+        return (mid.astype(F32) + added).astype(BF16)
 
     return jax.shard_map(device_step, mesh=mesh, in_specs=(row_spec, row_spec, row_spec, head_spec, head_spec, head_spec, out_spec, expert_spec, expert_spec, expert_spec), out_specs=row_spec, check_vma=False)

time: 94.1 us -> 95.3 us (1.013)
  other arithmetic: 0 us -> 2.05 us
  local copies, waits for them, and re-layouts: 1.77 us -> 0 us
    convert_element_type x0 -> x1, other arithmetic: none -> 2.05 us  [device_step(): return (mid.astype(F32) + added).astype(BF16)]
    unnamed x1 -> x0, local copies, waits for them, and re-layouts: 1.77 us -> none
where the time goes in v5:
time: 95.3 us; the launch traced here: 94.7 us
  Pallas kernels  92.6 us (97%)
  other arithmetic  2.05 us (2%)
    pallas_call x1, Pallas kernels, device_step(): pl.pallas_call(functools.partial(layer_kernel, dims), out_shape=[jax.Shap...  92.6 us
    convert_element_type x1, other arithmetic, device_step(): return (mid.astype(F32) + added).astype(BF16)  2.05 us

profile of v5, /device:TPU:97, one launch (start us, length us, event | category | flops | bytes accessed | tf_op | source)
XLA Modules:
  0.0 94.7 jit_solution(13713558089282866787)
XLA Ops:
  0.0 92.6 %layer.1 = (bf16[2,64,1536]{2,1,0:T(8,128)(2,1)}, f32[2,64,1536]{2,1,0:T(8,128)}) custom-call(bf16[2,64,1536]{2,1,0:T(8,128)(2,1)} %x_hbm.1, s32[2,2,64]{2,1,0:T(2,128)} %bitcast.22, f32[2,2,64]{2,1,0:T(2,128)} %bitcast.23, bf16[192,1536]{1,0:T(8,128)(2,1)} %bitcast.18, bf16[64,1536]{1,0:T(8,128)(2,1)} %bitcast.20, bf16[64,1536]{1,0:T(8,128)(2,1)} %bitcast.21, ...), custom_call_target="tpu_custom_call" | custom-call | tf_op jit(solution)/shard_map/layer/pallas_call | solution.py:518
  92.6 2.0 %add_convert_fusion = bf16[2,64,1536]{2,1,0:T(8,128)(2,1)} fusion(f32[2,64,1536]{2,1,0:T(8,128)} %get-tuple-element.8, bf16[2,64,1536]{2,1,0:T(8,128)(2,1)} %get-tuple-element.7), kind=kLoop, calls=%fused_computation | loop fusion | flops 589824 | bytes 1572864 | tf_op jit(solution)/shard_map/convert_element_type | solution.py:527

commit v6 on v4

--- a/solution.py
+++ b/solution.py
@@ -122,7 +122,13 @@
         return pl.ds(pl.multiple_of(hid - cps * unit + r * unit, unit), unit)
 
     wa = gather(lambda sl, part: wof.at[sl[0], sl[1], wparts[part], cols_a], ws_sem.at[0], wr_sem.at[0])
-    wb = gather(lambda sl, part: wof.at[sl[0], sl[1], wparts[part], cols_b(c)], ws_sem.at[1], wr_sem.at[1])
+
+    def wb(q, mine):
+        sl = own if mine else (left, right, opposite)[q]
+        ref = wof.at[sl[0], sl[1], :, cols_b(c)]
+        dst = (right, left, opposite)[q]
+        return rcopy(ref, ref, ws_sem.at[1, q], wr_sem.at[1, q], c, flat(dst))
+
 
     remote = (left, right, opposite)
 
@@ -220,7 +226,8 @@
         for cp in ld_qkv:
             cp.wait()
         ld_wo.wait()
-        wb[0](0, 2, 1, 3)
+        for q in range(3):
+            wb(q, True).start()
         wa[0](0, 2, 1, 3)
         share(0, True).start()
         got(6, 7, 8, 9, 10)
@@ -319,12 +326,23 @@
                     kv_copy(s, 1, c, r).wait_recv()
 
     def exchange(src, dst, ss, rs):
-        def go(i, _):
-            g = (me + i) % group
-            rcopy(src.at[g], dst.at[me], ss, rs, g // tps, g % tps).start()
+        def go(r, _):
+            for a, dx in enumerate((1, chips - 1, 2, 0)):
+                cc = (c + r + a) % cps
+                for dk in range(2):
+                    tt = flat(slot(dx, dk == 1))
+                    g = cc * tps + tt
+
+                    def send(g=g, cc=cc, tt=tt):
+                        rcopy(src.at[g], dst.at[me], ss, rs, cc, tt).start()
+
+                    if dx == 0 and dk == 0:
+                        pl.when(r != (cps - a) % cps)(send)
+                    else:
+                        send()
             return 0
 
-        lax.fori_loop(1, group, go, 0)
+        lax.fori_loop(0, cps, go, 0)
         dst[me] = src[me]
 
     def arrived(dst, rs):
@@ -340,43 +358,32 @@
             src = (t + i) % tps
             rcopy(orecv.at[s, src], orecv.at[s, src], os_sem.at[s, src], or_sem.at[s, src], c, src).wait_recv()
         total = xf[s, xc, core].astype(F32)
-        added = None
-        for u in range(tps):
-            term = mm(orecv[s, u][:, :kdim], wof[u // 2, u % 2])
-            added = term if added is None else added + term
+        rows = jnp.concatenate([orecv[s, u][:, :kdim] for u in range(tps)], axis=1)
+        added = mm(rows, wof[...].reshape(tps * kdim, hid))
         mid_rows = (total + added).astype(BF16)
         hbuf[s] = mid_rows
         dsend[s] = mm(onehot[s], mid_rows).reshape(group, cap, hid).astype(BF16)
         exchange(dsend.at[s], drecv.at[s], ds_sem.at[s], dr_sem.at[s])
 
     with scope('wb1'):
-        wb[1](0)
-        wb[0](4)
-        wb[1](2)
-        wb[0](5)
-        wb[1](1, 3)
-        for q in range(2):
+        for q in range(3):
+            wb(q, False).wait_recv()
             for i in range(1, cps):
                 spread(q, (c + i) % cps, c).start()
+            share(5 + q, True).start()
     with scope('kvwait00'):
         kv_wait(0, 0)
     with scope('attend00'):
         attend(0, 0)
-    with scope('wb2'):
-        wb[1](4, 5)
-        for i in range(1, cps):
-            spread(2, (c + i) % cps, c).start()
-        for k in (5, 6, 7):
-            share(k, True).start()
-        wa[1](0)
-        wa[0](4)
-        wa[1](2)
-        wa[0](5)
     with scope('kvwait01'):
         kv_wait(0, 1)
     with scope('attend01'):
         attend(0, 1)
     with scope('wa2'):
+        wa[1](0)
+        wa[0](4)
+        wa[1](2)
+        wa[0](5)
         wa[1](1, 3)
         share(1, True).start()
         share(2, True).start()
@@ -440,8 +447,9 @@
             rcopy(osend.at[s, dst], orecv.at[s, t], os_sem.at[s, dst], or_sem.at[s, t], c, dst).wait_send()
         left_all(dsend.at[s], ds_sem.at[s])
         left_all(rsend.at[s], rs_sem.at[s])
-    for part in (wa, wb):
-        part[2](*range(6))
+    wa[2](*range(6))
+    for q in range(3):
+        wb(q, True).wait_send()
     for q in range(3):
         for i in range(1, cps):
             spread(q, (c + i) % cps, c).wait_send()

time: 94.1 us -> 91.8 us (0.976)
  Pallas kernels: 92.2 us -> 89.8 us
    pallas_call x1, Pallas kernels: 92.2 us -> 89.8 us  [device_step(): pl.pallas_call(functools.partial(layer_kernel, dims), out_shape=jax.Shape...]
where the time goes in v6:
time: 91.8 us; the launch traced here: 91.6 us
  Pallas kernels  89.8 us (98%)
  local copies, waits for them, and re-layouts  1.77 us (2%)
    pallas_call x1, Pallas kernels, device_step(): pl.pallas_call(functools.partial(layer_kernel, dims), out_shape=jax.Shape...  89.8 us

profile of v6, /device:TPU:97, one launch (start us, length us, event | category | flops | bytes accessed | tf_op | source)
XLA Modules:
  0.0 91.6 jit_solution(4842830609093317109)
XLA Ops:
  0.0 89.8 %layer.1 = bf16[2,64,1536]{2,1,0:T(8,128)(2,1)} custom-call(bf16[2,64,1536]{2,1,0:T(8,128)(2,1)} %x_hbm.1, s32[2,2,64]{2,1,0:T(2,128)} %bitcast.22, f32[2,2,64]{2,1,0:T(2,128)} %bitcast.23, bf16[192,1536]{1,0:T(8,128)(2,1)} %bitcast.18, bf16[64,1536]{1,0:T(8,128)(2,1)} %bitcast.20, bf16[64,1536]{1,0:T(8,128)(2,1)} %bitcast.21, bf16[192,1536]{1,0:T(8,128)(2,1)} %bitcast.19, ...), custom_call_target="tpu_custom_call" | custom-call | tf_op jit(solution)/shard_map/layer/pallas_call | solution.py:521
  89.9 1.8 %copy.12 = bf16[2,64,1536]{2,1,0:T(8,128)(2,1)} copy(bf16[2,64,1536]{2,1,0:T(8,128)(2,1)} %layer.1) | data formatting | bytes 786432
